TPU v7x, 32 devices: a whole 2x2x4 slice. The times are simulated.
32 devices in a mesh: dp: 8 (over z, x), hyper: 4 (over y, core).
Axes of the slice: x: 2, y: 2, z: 4, core: 2. Of those that a mesh axis runs over, the one named last changes fastest.
Arguments:
- inputs: bfloat16 [64, 64, 128], P(('dp', 'hyper')), may hold values from -64 to 64
- labels: int32 [64, 64], P(('dp', 'hyper')), may hold values from 0 to 255
- client_ids: int32 [64], P(('dp', 'hyper')), may hold values from 0 to 63
- ext_weight: bfloat16 [128, 4096], replicated, may hold values from -0.5 to 0.5
- ext_bias: bfloat16 [4096], replicated, may hold values from -3 to 3
- embeddings: bfloat16 [64, 128], replicated, may hold values from -1.5 to 1.5
- hyper_in: bfloat16 [128, 50], replicated, may hold values from -2.09375 to 2.09375
- hyper_bias: float32 [50], replicated, may hold values from -3 to 3
- hyper_out: bfloat16 [4096, 50, 256], P('hyper'), may hold values from -0.1796875 to 0.1796875
Outputs:
- grad_ext_weight: float32 [128, 4096], replicated
- grad_ext_bias: float32 [4096], replicated
- grad_embeddings: float32 [64, 128], replicated
- grad_hyper_in: float32 [128, 50], replicated
- grad_hyper_bias: float32 [50], replicated
- grad_hyper_out: float32 [4096, 50, 256], P(('hyper', 'dp'))
Inputs may be any that keep to these rules, and one draw needn't show every extreme that they name: `client_ids`: A client may hold several slots or none.
All inputs are finite; a program needn't handle non-finite values.
Results may differ from a plain program's by a relative error of at most 0.014.
The roundings to bfloat16 on the way count: a program that leaves them out, or rounds other values in their place, can miss the bound.
Values may be sent and summed in bfloat16 or wider, within the bound.
A program may use at most 192 MiB of HBM per device.

v0:
```python
import jax
import jax.numpy as jnp
from jax import lax
from jax.sharding import PartitionSpec as P

highest = lax.Precision.HIGHEST


def silu_slope(values):
    logistic = jax.nn.sigmoid(values)
    return logistic * (1.0 + values * (1.0 - logistic))


def class_grads(logits, slot_labels, row_count):
    largest = jnp.max(logits, axis=-1, keepdims=True)
    exponent = jnp.exp(logits - largest)
    probability = exponent / jnp.sum(exponent, axis=-1, keepdims=True)
    classes = jnp.arange(logits.shape[-1], dtype=jnp.int32)
    onehot = (slot_labels[..., None] == classes).astype(jnp.float32)
    return ((probability - onehot) / row_count).astype(jnp.bfloat16)


def local(
    inputs, labels, client_ids, ext_weight, ext_bias, embeddings, hyper_in, hyper_bias, hyper_out
):
    slot_count, row_count, width_in = inputs.shape
    width = ext_weight.shape[1]
    flat_in = inputs.reshape(slot_count * row_count, width_in)
    preact = jnp.dot(flat_in, ext_weight, preferred_element_type=jnp.float32) + ext_bias.astype(
        jnp.float32
    )
    features = jax.nn.silu(preact).astype(jnp.bfloat16).reshape(slot_count, row_count, width)
    row_ids = lax.all_gather(client_ids, "hyper", axis=0, tiled=True)
    table_ids = jnp.arange(embeddings.shape[0], dtype=jnp.int32)
    select = (row_ids[:, None] == table_ids[None, :]).astype(jnp.bfloat16)
    picked = jnp.dot(select, embeddings, preferred_element_type=jnp.float32).astype(jnp.bfloat16)
    hyper_preact = jnp.dot(picked, hyper_in, preferred_element_type=jnp.float32) + hyper_bias
    hidden = jax.nn.silu(hyper_preact).astype(jnp.bfloat16)
    head_part = jnp.einsum(
        "kh,dhc->kdc", hidden, hyper_out, preferred_element_type=jnp.float32
    ).astype(jnp.bfloat16)
    client_heads = lax.all_to_all(head_part, "hyper", split_axis=0, concat_axis=1, tiled=True)
    logits = jnp.einsum("krd,kdc->krc", features, client_heads, preferred_element_type=jnp.float32)
    dlogits = class_grads(logits, labels, row_count)
    dheads_own = jnp.einsum(
        "krd,krc->kdc", features, dlogits, preferred_element_type=jnp.float32
    ).astype(jnp.bfloat16)
    dfeatures = jnp.einsum(
        "krc,kdc->krd", dlogits, client_heads, preferred_element_type=jnp.float32
    ).astype(jnp.bfloat16)
    dhead_part = lax.all_to_all(dheads_own, "hyper", split_axis=1, concat_axis=0, tiled=True)
    dpreact = (
        dfeatures.reshape(slot_count * row_count, width).astype(jnp.float32) * silu_slope(preact)
    ).astype(jnp.bfloat16)
    grad_weight = jnp.dot(flat_in.T, dpreact, preferred_element_type=jnp.float32)
    grad_bias = jnp.sum(dpreact.astype(jnp.float32), axis=0)
    grad_out = lax.psum_scatter(
        jnp.einsum("kh,kdc->dhc", hidden, dhead_part, preferred_element_type=jnp.float32).astype(
            jnp.bfloat16
        ),
        "dp",
        scatter_dimension=0,
        tiled=True,
    ).astype(jnp.float32)
    dhidden = jnp.einsum("kdc,dhc->kh", dhead_part, hyper_out, preferred_element_type=jnp.float32)
    hyper_dpre = dhidden * silu_slope(hyper_preact)
    grad_in = jnp.dot(picked.astype(jnp.float32).T, hyper_dpre, precision=highest)
    grad_hbias = jnp.sum(hyper_dpre, axis=0)
    back_rows = jnp.dot(hyper_dpre, hyper_in.astype(jnp.float32).T, precision=highest)
    grad_table = jnp.dot(select.astype(jnp.float32).T, back_rows, precision=highest)
    grad_weight, grad_bias, grad_table, grad_in, grad_hbias = lax.psum(
        (grad_weight, grad_bias, grad_table, grad_in, grad_hbias), ("dp", "hyper")
    )
    return (grad_weight, grad_bias, grad_table, grad_in, grad_hbias, grad_out)


def solution(mesh):
    placed = (
        P(("dp", "hyper"), None, None),
        P(("dp", "hyper"), None),
        P(("dp", "hyper")),
        P(),
        P(),
        P(),
        P(),
        P(),
        P("hyper", None, None),
    )
    return jax.shard_map(
        local,
        mesh=mesh,
        in_specs=placed,
        out_specs=(P(), P(), P(), P(), P(), P(("hyper", "dp"), None, None)),
        check_vma=False,
    )
```

profile of v0, /device:TPU:0, one launch (start us, length us, event | category | flops | bytes accessed | tf_op | source)
XLA Modules:
  0.0 719.1 jit_solution(14402393929329942820)
XLA Ops:
  8.0 0.0 copy-start
  8.0 1.3 dynamic-slice
  10.0 0.9 dynamic-update-slice
  10.9 6.4 all-reduce
  17.3 0.9 convolution_convert_fusion.2
  18.2 0.8 convolution_add_fusion.1
  19.0 27.9 %fusion.4 = bf16[8,1024,256]{2,0,1:T(8,128)(2,1)S(1)} fusion(bf16[1024,50,256]{2,0,1:T(8,128)(2,1)} %param.17, f32[8,50]{1,0:T(8,128)S(1)} %convolution_add_fusion.1), kind=kOutput, calls=%fused_computation.9 | convolution fusion | flops 211814352 | bytes 30410304 | tf_op jit(solution)/shard_map/kh,dhc->kdc/dot_general | solution.py:39
  46.9 2.9 copy.23
  49.8 5.0 all-to-all-start
  54.8 0.0 copy-done.5
  54.8 2.0 multiply_convert_fusion
  56.9 46.1 %all-to-all-done = bf16[8,1024,256]{2,1,0:T(8,128)(2,1)} async-done(((bf16[8,1024,256]{2,1,0:T(8,128)(2,1)}), bf16[8,1024,256]{2,1,0:T(8,128)(2,1)}, u32[]{:S(2)}, u32[]{:S(2)}) %all-to-all-start) | async-done | bytes 4194336 | tf_op jit(solution)/shard_map/all_to_all | solution.py:42
  103.0 2.5 copy.24
  105.5 0.0 copy-start.2
  105.5 0.0 copy-start.6
  105.5 2.0 copy-done.2
  107.5 0.8 fusion.32
  108.3 3.4 convolution_convert_fusion
  111.7 10.1 %copy.25 = bf16[2,4096,256]{2,0,1:T(2,128)(2,1)} copy(bf16[2,4096,256]{2,1,0:T(8,128)(2,1)} %convolution_convert_fusion) | data formatting | bytes 8388608 | tf_op jit(solution)/shard_map/convert_element_type | solution.py:47
  121.8 4.8 all-to-all-start.1
  126.7 0.0 all-reduce.5.cloned.1.call-start
  126.7 3.7 convolution_convert_fusion.1
  130.4 3.1 convert_reduce_fusion
  133.5 1.8 convolution_bitcast_fusion
  135.3 0.0 all-reduce.5.cloned.1.call-update
  135.3 0.0 reduce-scatter.2.cloned.1.call-start
  135.4 45.1 %all-to-all-done.1 = bf16[2,4096,256]{2,0,1:T(2,128)(2,1)} async-done(((bf16[2,4096,256]{2,0,1:T(2,128)(2,1)}), bf16[2,4096,256]{2,0,1:T(2,128)(2,1)}, u32[]{:S(2)}, u32[]{:S(2)}) %all-to-all-start.1) | async-done | bytes 4194336 | tf_op jit(solution)/shard_map/all_to_all | solution.py:51
  180.5 15.9 %copy.26 = bf16[2,4,1024,256]{2,0,1,3:T(2,128)(2,1)} copy(bf16[2,4,1024,256]{3,0,2,1:T(2,128)(2,1)} %bitcast.9) | data formatting | bytes 8388608 | tf_op jit(solution)/shard_map/all_to_all | solution.py:51
  196.3 7.2 %all_to_all.33 = bf16[8,1024,256]{1,0,2:T(8,128)(2,1)} reshape(bf16[4,2,1024,256]{2,1,0,3:T(2,128)(2,1)} %bitcast.51) | data formatting | bytes 8388608 | tf_op jit(solution)/shard_map/all_to_all | solution.py:51
  203.5 7.3 %copy.28 = bf16[8,1024,256]{2,0,1:T(8,128)(2,1)} copy(bf16[8,1024,256]{1,0,2:T(8,128)(2,1)} %all_to_all.33) | data formatting | bytes 8388608 | tf_op jit(solution)/shard_map/all_to_all | solution.py:51
  210.8 14.4 %convert_bitcast_fusion = bf16[1024,50,256]{2,1,0:T(8,128)(2,1)} fusion(bf16[8,1024,256]{2,0,1:T(8,128)(2,1)} %copy.28, f32[8,50]{1,0:T(8,128)S(1)} %convolution_add_fusion.1), kind=kOutput, calls=%fused_computation.4 | convolution fusion | flops 222824400 | bytes 30410304 | tf_op jit(solution)/shard_map/kh,kdc->dhc/dot_general | solution.py:58
  225.1 0.0 reduce-scatter.2.cloned.1.call-update
  225.2 0.0 all-reduce.7.cloned.1.call-start
  225.2 40.0 %copy.27 = bf16[1024,50,256]{0,1,2:T(8,128)(2,1)} copy(bf16[1024,50,256]{2,0,1:T(8,128)(2,1)} %param.17) | data formatting | bytes 52428800 | tf_op args[8]
  265.3 14.6 %fusion.31 = (f32[50]{0:T(128)}, f32[8,50]{1,0:T(8,128)S(1)}) fusion(f32[8,50]{1,0:T(8,128)S(1)} %convolution_add_fusion.1, bf16[8,1024,256]{1,0,2:T(8,128)(2,1)} %all_to_all.33, bf16[1024,50,256]{0,1,2:T(8,128)(2,1)} %copy.27), kind=kOutput, calls=%fused_computation.44 | convolution fusion | flops 209718752 | bytes 30412104 | tf_op jit(solution)/shard_map/kdc,dhc->kh/dot_general | solution.py:65
  279.9 0.1 fusion.33
  280.0 0.8 fusion.34
  280.8 0.9 fusion.21
  281.7 0.0 all-reduce.7.cloned.1.call-update
  281.8 136.2 %all-reduce.5.cloned.1.call-done = f32[128,4096]{0,1:T(8,128)} async-done(((f32[128,4096]{0,1:T(8,128)}), f32[128,4096]{0,1:T(8,128)}) %all-reduce.5.cloned.1.call-update) | async-done | bytes 2097168 | tf_op jit(solution)/shard_map/psum | solution.py:71
  418.0 3.0 copy.29
  421.0 279.0 %reduce-scatter.2.cloned.1.call-done = bf16[128,50,256]{2,1,0:T(8,128)(2,1)} async-done(((bf16[1024,50,256]{2,1,0:T(8,128)(2,1)}), bf16[128,50,256]{2,1,0:T(8,128)(2,1)}) %reduce-scatter.2.cloned.1.call-update) | async-done | bytes 3276816 | tf_op jit(solution)/shard_map/reduce_scatter | solution.py:57
  699.9 5.7 copy.30
  705.6 0.8 all-reduce.7.cloned.1.call-done
  706.5 1.3 copy.41
  707.8 1.4 copy.42
  709.2 1.4 copy.43
  710.5 1.2 copy.44
  (11 shorter events, 0.0 us)
Async XLA Ops:
  8.0 46.8 %copy-start = (bf16[128,4096]{1,0:T(8,128)(2,1)S(1)}, bf16[128,4096]{1,0:T(8,128)(2,1)}, u32[]{:S(2)}) copy-start(bf16[128,4096]{1,0:T(8,128)(2,1)} %param.12) | copy-start | bytes 3145732
  49.8 5.0 copy-start.5
  49.8 5.0 copy-start.4
  49.8 53.2 %all-to-all-start = ((bf16[8,1024,256]{2,1,0:T(8,128)(2,1)}), bf16[8,1024,256]{2,1,0:T(8,128)(2,1)}, u32[]{:S(2)}, u32[]{:S(2)}) async-start(bf16[8,1024,256]{2,1,0:T(8,128)(2,1)} %copy.23), calls=%async_computation | async-start | bytes 8388608 | tf_op jit(solution)/shard_map/all_to_all | solution.py:42
  105.5 2.0 copy-start.2
  105.5 2.8 copy-start.6
  121.8 58.7 %all-to-all-start.1 = ((bf16[2,4096,256]{2,0,1:T(2,128)(2,1)}), bf16[2,4096,256]{2,0,1:T(2,128)(2,1)}, u32[]{:S(2)}, u32[]{:S(2)}) async-start(bf16[2,4096,256]{2,0,1:T(2,128)(2,1)} %copy.25), calls=%async_computation.1 | async-start | bytes 8388608 | tf_op jit(solution)/shard_map/all_to_all | solution.py:51
  126.7 291.3 %all-reduce.5.cloned.1.call-start = ((), (), s32[]{:S(2)}) async-start(), calls=%async_computation.3 | async-start | bytes 4194304 | tf_op jit(solution)/shard_map/psum | solution.py:71
  135.3 564.6 %reduce-scatter.2.cloned.1.call-start = ((), (), s32[]{:S(2)}) async-start(), calls=%async_computation.4 | async-start | bytes 33030144 | tf_op jit(solution)/shard_map/reduce_scatter | solution.py:57
  225.2 481.3 %all-reduce.7.cloned.1.call-start = ((), (), s32[]{:S(2)}) async-start(), calls=%async_computation.5 | async-start | bytes 156672 | tf_op jit(solution)/shard_map/psum | solution.py:71
  265.3 14.6 %copy-start.3 = (bf16[128,50]{0,1:T(8,128)(2,1)S(1)}, bf16[128,50]{0,1:T(8,128)(2,1)}, u32[]{:S(2)}) copy-start(bf16[128,50]{0,1:T(8,128)(2,1)} %param.15) | copy-start | bytes 38404
  418.0 293.7 %copy-start.1 = (bf16[128,4096]{1,0:T(8,128)(2,1)S(1)}, bf16[128,4096]{1,0:T(8,128)(2,1)}, u32[]{:S(2)}) copy-start(bf16[128,4096]{1,0:T(8,128)(2,1)} %param.12) | copy-start | bytes 3145732
Sparse Core Ops, SparseCore 0:
  135.5 282.4 all-reduce.4
  424.7 281.7 all-reduce.6
Sparse Core Ops, SparseCore 1:
  225.2 474.6 reduce-scatter.1
where the time goes:
time: 722 us; the launch traced here: 719 us
  waiting for transfers between devices  507 us (70%)
  local copies, waits for them, and re-layouts  104 us (14%)
  matrix products  72.3 us (10%)
  between operations  16.3 us (2%)
  starting transfers between devices  9.96 us (1%)
    reduce_scatter x1, waiting for transfers between devices, local(): lax.psum_scatter(jnp.einsum('kh,kdc->dhc', hidden, dhead_part, preferred_...  279 us
    psum x2, waiting for transfers between devices, local(): lax.psum((grad_weight, grad_bias, grad_table, grad_in, grad_hbias), ('dp'...  137 us
    unnamed x24, local copies, waits for them, and re-layouts  58.1 us
    all_to_all x1, waiting for transfers between devices, local(): lax.all_to_all(head_part, 'hyper', split_axis=0, concat_axis=1, tiled=True)  46.1 us
    all_to_all x1, waiting for transfers between devices, local(): lax.all_to_all(dheads_own, 'hyper', split_axis=1, concat_axis=0, tiled=True)  45.1 us
    all_to_all x3, local copies, waits for them, and re-layouts, local(): lax.all_to_all(dheads_own, 'hyper', split_axis=1, concat_axis=0, tiled=True)  30.3 us
    dot_general x1, matrix products, local(): jnp.einsum('kh,dhc->kdc', hidden, hyper_out, preferred_element_type=jnp.f...  27.9 us
    dot_general x1, matrix products, local(): jnp.einsum('kdc,dhc->kh', dhead_part, hyper_out, preferred_element_type=j...  14.6 us
  transfers between devices with their start and end apart: 5, of which 5 were waited for; matrix products, arithmetic and copies ran while one was open for 16% of the time, Pallas kernels for 0%

commit v1 on v0

v1 whole, which is shorter than its diff:
```python
import jax
import jax.numpy as jnp
from jax import lax
from jax.sharding import PartitionSpec as P

highest = lax.Precision.HIGHEST
f32 = jnp.float32
bf16 = jnp.bfloat16


def silu_slope(values):
    logistic = jax.nn.sigmoid(values)
    return logistic * (1.0 + values * (1.0 - logistic))


def class_grads(logits, slot_labels, row_count):
    largest = jnp.max(logits, axis=-1, keepdims=True)
    exponent = jnp.exp(logits - largest)
    probability = exponent / jnp.sum(exponent, axis=-1, keepdims=True)
    classes = jnp.arange(logits.shape[-1], dtype=jnp.int32)
    onehot = (slot_labels[..., None] == classes).astype(f32)
    return ((probability - onehot) / row_count).astype(bf16)


def local(
    inputs, labels, client_ids, ext_weight, ext_bias, embeddings, hyper_in, hyper_bias, hyper_out
):
    everyone = ("dp", "hyper")
    n_dp, n_hyper = lax.axis_size("dp"), lax.axis_size("hyper")
    i, j = lax.axis_index("dp"), lax.axis_index("hyper")
    own, rows, width_in = inputs.shape
    wide = hyper_out.shape[0]
    narrow = wide // n_dp
    group = own * n_hyper
    slots = group * n_dp
    classes = hyper_out.shape[2]

    ids = lax.all_gather(client_ids, everyone, axis=0, tiled=True)
    in_group = lax.all_gather(inputs, "hyper", axis=0, tiled=True)
    in_all = lax.all_gather(in_group, "dp", axis=0, tiled=True)
    select = (ids[:, None] == jnp.arange(embeddings.shape[0], dtype=jnp.int32)[None, :])
    picked = jnp.dot(select.astype(bf16), embeddings, preferred_element_type=f32).astype(bf16)
    hyper_preact = jnp.dot(picked, hyper_in, preferred_element_type=f32) + hyper_bias
    hidden = jax.nn.silu(hyper_preact).astype(bf16)

    w_wide = lax.dynamic_slice_in_dim(ext_weight, j * wide, wide, 1)
    b_wide = lax.dynamic_slice_in_dim(ext_bias, j * wide, wide, 0).astype(f32)
    preact = jnp.dot(in_group.reshape(group * rows, width_in), w_wide, preferred_element_type=f32)
    features = jax.nn.silu(preact + b_wide).astype(bf16).reshape(group, rows, wide)
    hidden_group = lax.dynamic_slice_in_dim(hidden, i * group, group, 0)
    heads = jnp.einsum("kh,dhc->kdc", hidden_group, hyper_out, preferred_element_type=f32)
    part = jnp.einsum("krd,kdc->krc", features, heads.astype(bf16), preferred_element_type=f32)
    parts = lax.all_to_all(
        part.reshape(n_hyper, own * rows, classes), "hyper", split_axis=0, concat_axis=0
    )
    logits = jnp.sum(parts, axis=0).reshape(own, rows, classes)
    dlogits = class_grads(logits, labels, rows)
    dl_all = lax.all_gather(dlogits, everyone, axis=0, tiled=True)

    start = (j * n_dp + i) * narrow
    w = lax.dynamic_slice_in_dim(ext_weight, start, narrow, 1)
    b = lax.dynamic_slice_in_dim(ext_bias, start, narrow, 0).astype(f32)
    out_rows = lax.dynamic_slice_in_dim(hyper_out, i * narrow, narrow, 0)
    flat = in_all.reshape(slots * rows, width_in)
    preact = jnp.dot(flat, w, preferred_element_type=f32) + b
    features = jax.nn.silu(preact).astype(bf16).reshape(slots, rows, narrow)
    heads = jnp.einsum("kh,dhc->kdc", hidden, out_rows, preferred_element_type=f32).astype(bf16)
    dheads = jnp.einsum("krd,krc->kdc", features, dl_all, preferred_element_type=f32).astype(bf16)
    dfeatures = jnp.einsum("krc,kdc->krd", dl_all, heads, preferred_element_type=f32).astype(bf16)
    dpreact = (
        dfeatures.reshape(slots * rows, narrow).astype(f32) * silu_slope(preact)
    ).astype(bf16)
    grad_weight = jnp.dot(flat.T, dpreact, preferred_element_type=f32)
    grad_bias = jnp.sum(dpreact.astype(f32), axis=0)
    grad_out = jnp.einsum("kh,kdc->dhc", hidden, dheads, preferred_element_type=f32)
    dhidden = jnp.einsum("kdc,dhc->kh", dheads, out_rows, preferred_element_type=f32)
    dhidden = lax.psum(dhidden, everyone)
    hyper_dpre = dhidden * silu_slope(hyper_preact)
    grad_in = jnp.dot(picked.astype(f32).T, hyper_dpre, precision=highest)
    grad_hbias = jnp.sum(hyper_dpre, axis=0)
    back_rows = jnp.dot(hyper_dpre, hyper_in.astype(f32).T, precision=highest)
    grad_table = jnp.dot(select.astype(f32).T, back_rows, precision=highest)
    both = jnp.concatenate([grad_weight, grad_bias[None]], axis=0)
    both = lax.all_gather(both, ("hyper", "dp"), axis=1, tiled=True)
    return (both[:-1], both[-1], grad_table, grad_in, grad_hbias, grad_out)


def solution(mesh):
    placed = (
        P(("dp", "hyper"), None, None),
        P(("dp", "hyper"), None),
        P(("dp", "hyper")),
        P(),
        P(),
        P(),
        P(),
        P(),
        P("hyper", None, None),
    )
    return jax.shard_map(
        local,
        mesh=mesh,
        in_specs=placed,
        out_specs=(P(), P(), P(), P(), P(), P(("hyper", "dp"), None, None)),
        check_vma=False,
    )
```

time: 722 us -> 277 us (0.38)
  waiting for transfers between devices: 507 us -> 55.1 us
  blocking collectives: 6.41 us -> 98.8 us
  local copies, waits for them, and re-layouts: 104 us -> 42.4 us
  matrix products: 72.3 us -> 61.7 us
  starting transfers between devices: 9.96 us -> 0.12 us
    reduce_scatter x1 -> x0, waiting for transfers between devices: 279 us -> none  [local(): lax.psum_scatter(jnp.einsum('kh,kdc->dhc', hidden, dhead_part, preferred_...]
    psum x2 -> x0, waiting for transfers between devices: 137 us -> none  [local(): lax.psum((grad_weight, grad_bias, grad_table, grad_in, grad_hbias), ('dp'...]
    all_to_all x2 -> x0, waiting for transfers between devices: 91.2 us -> none  [the longest x1 46.1 us: local(): lax.all_to_all(head_part, 'hyper', split_axis=0, concat_axis=1, tiled=True)]
    all_gather x0 -> x3, waiting for transfers between devices: none -> 54.3 us  [the longest x1 33.7 us: local(): in_all = lax.all_gather(in_group, 'dp', axis=0, tiled=True)]
    psum x0 -> x1, blocking collectives: none -> 39.1 us  [local(): dhidden = lax.psum(dhidden, everyone)]
    unnamed x1, blocking collectives: 6.41 us -> 42 us
    all_to_all x4 -> x0, local copies, waits for them, and re-layouts: 32.8 us -> none  [the longest x3 30.3 us: local(): lax.all_to_all(dheads_own, 'hyper', split_axis=1, concat_axis=0, tiled=True)]
    unnamed x24 -> x16, local copies, waits for them, and re-layouts: 58.1 us -> 33.5 us
  transfers between devices with their start and end apart: 5 -> 3, of which waited for: 5 -> 2; matrix products, arithmetic and copies ran while one was open for 16% -> 23% of each run, Pallas kernels for 0% -> 0%
where the time goes in v1:
time: 277 us; the launch traced here: 276 us
  blocking collectives  98.8 us (36%)
  matrix products  61.7 us (22%)
  waiting for transfers between devices  55.1 us (20%)
  local copies, waits for them, and re-layouts  42.4 us (15%)
  between operations  13.9 us (5%)
  other arithmetic  4 us (1%)
    unnamed x1, blocking collectives  42 us
    psum x1, blocking collectives, local(): dhidden = lax.psum(dhidden, everyone)  39.1 us
    all_gather x1, waiting for transfers between devices, local(): in_all = lax.all_gather(in_group, 'dp', axis=0, tiled=True)  33.7 us
    unnamed x16, local copies, waits for them, and re-layouts  33.5 us
    dot_general x1, matrix products, local(): jnp.einsum('kh,dhc->kdc', hidden_group, hyper_out, preferred_element_type...  28 us
    all_gather x1, waiting for transfers between devices, local(): dl_all = lax.all_gather(dlogits, everyone, axis=0, tiled=True)  20.6 us
    all_to_all x1, blocking collectives, local(): lax.all_to_all(part.reshape(n_hyper, own * rows, classes), 'hyper', split...  11.8 us
    dot_general x1, matrix products, local(): jnp.einsum('kdc,dhc->kh', dheads, out_rows, preferred_element_type=f32)  7.1 us
  transfers between devices with their start and end apart: 3, of which 2 were waited for; matrix products, arithmetic and copies ran while one was open for 23% of the time, Pallas kernels for 0%

profile of v1, /device:TPU:0, one launch (start us, length us, event | category | flops | bytes accessed | tf_op | source)
XLA Modules:
  0.0 276.0 jit_solution(7571744221663631513)
XLA Ops:
  7.2 0.0 copy-start
  7.2 0.0 all-gather.4.cloned.1.call-start
  7.2 0.9 dynamic-update-slice
  8.2 42.0 %all-reduce = s32[64]{0:T(128)S(1)} all-reduce(s32[64]{0:T(128)S(1)} %dynamic-update-slice), channel_id=1, replica_groups=mesh['dp'=8,'hyper'=4] {'dp','hyper'}, use_global_device_ids=true, to_apply=%add | all-reduce | flops 64 | bytes 512
  50.1 6.0 %all_gather.15 = bf16[8,64,128]{2,1,0:T(8,128)(2,1)S(1)} all-gather(bf16[2,64,128]{2,1,0:T(8,128)(2,1)} %param.9), channel_id=1, replica_groups=mesh['dp'=8,'hyper'=4] {'hyper'}, dimensions={0}, use_global_device_ids=true | all-gather | bytes 163840 | tf_op jit(solution)/shard_map/all_gather | solution.py:39
  56.1 0.7 dynamic-slice_convert_fusion
  56.8 0.9 convolution_convert_fusion.2
  57.7 0.9 multiply_convert_fusion.3
  58.6 0.0 copy-done
  58.6 0.7 fusion.21
  59.4 0.0 copy-done.3
  59.4 28.0 %convolution_convert_fusion.1 = bf16[8,1024,256]{2,0,1:T(8,128)(2,1)S(1)} fusion(bf16[64,50]{0,1:T(8,128)(2,1)S(1)} %get-tuple-element.29, s32[]{:T(128)S(6)} %select_n.15, bf16[1024,50,256]{2,0,1:T(8,128)(2,1)} %param.17), kind=kOutput, calls=%fused_computation.16 | convolution fusion | flops 211812352 | bytes 30415108 | tf_op jit(solution)/shard_map/kh,dhc->kdc/dot_general | solution.py:51
  87.4 0.0 copy-start.5
  87.4 0.9 fusion.3
  88.2 11.8 %all_to_all.5 = f32[4,128,256]{2,1,0:T(8,128)S(1)} all-to-all(f32[4,128,256]{2,1,0:T(8,128)S(1)} %bitcast.61), channel_id=1, replica_groups=mesh['dp'=8,'hyper'=4] {'hyper'}, dimensions={0} | all-to-all | bytes 1048576 | tf_op jit(solution)/shard_map/all_to_all | solution.py:53
  100.0 0.1 reduce_max.9
  100.1 0.2 exponential_reduce_fusion
  100.3 0.1 sub.24
  100.4 0.1 div.32
  100.5 0.8 multiply_convert_fusion.2
  101.3 0.0 all-gather.4.cloned.1.call-update
  101.3 0.0 all-gather.6.cloned.1.call-start
  101.3 0.7 all-gather.6.cloned.1.call-update
  102.0 0.0 all-gather.8.cloned.1.call-start
  102.1 27.8 %copy.28 = bf16[1024,50,256]{2,1,0:T(8,128)(2,1)} copy(bf16[1024,50,256]{2,0,1:T(8,128)(2,1)} %param.17) | data formatting | bytes 52428800 | tf_op args[8]
  129.9 0.8 dynamic-slice_convert_fusion.1
  130.6 5.3 %fusion.15 = bf16[64,128,256]{2,0,1:T(8,128)(2,1)} fusion(bf16[1024,50,256]{2,1,0:T(8,128)(2,1)} %copy.28, s32[]{:T(128)S(6)} %select_n.16, bf16[64,50]{0,1:T(8,128)(2,1)S(1)} %get-tuple-element.29), kind=kOutput, calls=%fused_computation.14 | convolution fusion | flops 211812352 | bytes 7870724 | tf_op jit(solution)/shard_map/kh,dhc->kdc/dot_general | solution.py:67
  136.0 20.6 %all-gather.4.cloned.1.call-done = bf16[64,64,256]{2,1,0:T(8,128)(2,1)} async-done(((bf16[2,64,256]{2,1,0:T(8,128)(2,1)}), bf16[64,64,256]{2,1,0:T(8,128)(2,1)}) %all-gather.4.cloned.1.call-update) | async-done | bytes 2097168 | tf_op jit(solution)/shard_map/all_gather | solution.py:58
  156.5 5.5 %fusion.22 = bf16[64,64,128]{2,1,0:T(8,128)(2,1)S(1)} fusion(bf16[64,64,256]{2,1,0:T(8,128)(2,1)} %all-gather.4.cloned.1.call-done, bf16[64,128,256]{2,0,1:T(8,128)(2,1)} %fusion.15), kind=kOutput, calls=%fused_computation.27 | convolution fusion | flops 268959744 | bytes 7340032 | tf_op jit(solution)/shard_map/krc,kdc->krd/dot_general | solution.py:69
  162.1 0.2 bitcast_convert_fusion
  162.3 1.8 copy.32
  164.1 33.7 %all-gather.6.cloned.1.call-done = bf16[64,64,128]{2,1,0:T(8,128)(2,1)} async-done(((bf16[8,64,128]{2,1,0:T(8,128)(2,1)}), bf16[64,64,128]{2,1,0:T(8,128)(2,1)}) %all-gather.6.cloned.1.call-update) | async-done | bytes 1048592 | tf_op jit(solution)/shard_map/all_gather | solution.py:40
  197.8 4.2 %convert_reduce_fusion = (f32[128]{0:T(128)S(1)}, bf16[4096,128]{0,1:T(8,128)(2,1)S(1)}, bf16[4096,128]{0,1:T(8,128)(2,1)}) fusion(f32[4096,128]{0,1:T(8,128)} %copy.32, f32[128]{0:T(128)S(1)} %dynamic-slice_convert_fusion.1, bf16[4096,128]{1,0:T(8,128)(2,1)} %bitcast.58, bf16[128,4096]{1,0:T(8,128)(2,1)S(1)} %copy-done, s32[]{:T(128)S(6)} %select_n.17), kind=kOutput, calls=%fused_computation.23 | convolution fusion | flops 141557632 | bytes 5276676 | tf_op jit(solution)/shard_map/dot_general | solution.py:65
  202.1 0.5 convolution_bitcast_fusion
  202.6 0.6 pad_maximum_fusion
  203.2 0.0 all-gather.8.cloned.1.call-update
  203.2 2.3 copy.33
  205.5 2.5 convolution_convert_fusion
  208.0 3.3 %fusion.12 = f32[128,50,256]{2,1,0:T(8,128)S(1)} fusion(bf16[64,128,256]{2,1,0:T(8,128)(2,1)S(1)} %convolution_convert_fusion, bf16[64,50]{0,1:T(8,128)(2,1)S(1)} %get-tuple-element.29), kind=kOutput, calls=%fused_computation.13 | convolution fusion | flops 209715200 | bytes 10754304 | tf_op jit(solution)/shard_map/kh,kdc->dhc/dot_general | solution.py:75
  211.3 4.8 %copy.37 = f32[128,50,256]{2,0,1:T(8,128)} copy(f32[128,50,256]{2,1,0:T(8,128)S(1)} %fusion.12) | data formatting | bytes 13107200
  216.1 7.1 %fusion.25 = f32[64,50]{0,1:T(8,128)S(1)} fusion(bf16[1024,50,256]{2,1,0:T(8,128)(2,1)} %copy.28, s32[]{:T(128)S(6)} %select_n.16, bf16[64,128,256]{2,1,0:T(8,128)(2,1)S(1)} %convolution_convert_fusion), kind=kOutput, calls=%fused_computation.29 | convolution fusion | flops 209715200 | bytes 7877124 | tf_op jit(solution)/shard_map/kdc,dhc->kh/dot_general | solution.py:76
  223.2 39.1 %psum.7 = f32[64,50]{0,1:T(8,128)S(1)} all-reduce(f32[64,50]{0,1:T(8,128)S(1)} %fusion.25), channel_id=1, replica_groups=mesh['dp'=8,'hyper'=4] {'dp','hyper'}, use_global_device_ids=true, to_apply=%region_4.5 | all-reduce | flops 3200 | bytes 25600 | tf_op jit(solution)/shard_map/psum | solution.py:77
  262.3 0.6 fusion.45
  263.0 0.2 fusion.46
  263.2 0.9 fusion.32
  264.1 0.8 fusion.47
  264.9 1.5 slice.9
  266.4 3.1 %slice.8 = f32[128,4096]{1,0:T(8,128)} slice(f32[129,4096]{1,0:T(8,128)} %all-gather.8.cloned.1.call-done), slice={[0:128], [0:4096]} | slice | bytes 4194304 | tf_op jit(solution)/shard_map/slice | solution.py:85
  (11 shorter events, 0.1 us)
Async XLA Ops:
  7.2 51.5 %copy-start = (bf16[128,4096]{1,0:T(8,128)(2,1)S(1)}, bf16[128,4096]{1,0:T(8,128)(2,1)}, u32[]{:S(2)}) copy-start(bf16[128,4096]{1,0:T(8,128)(2,1)} %param.12) | copy-start | bytes 3145732
  7.2 149.4 %all-gather.4.cloned.1.call-start = ((), (), s32[]{:S(2)}) async-start(), calls=%async_computation.1 | async-start | bytes 2162688 | tf_op jit(solution)/shard_map/all_gather | solution.py:58
  56.1 3.2 %copy-start.3 = (bf16[8,64,128]{2,1,0:T(8,128)(2,1)}, bf16[8,64,128]{2,1,0:T(8,128)(2,1)S(1)}, u32[]{:S(2)}) copy-start(bf16[8,64,128]{2,1,0:T(8,128)(2,1)S(1)} %all_gather.15) | copy-start | bytes 393220
  87.4 13.1 %copy-start.5 = (s32[2,64]{1,0:T(2,128)S(1)}, s32[2,64]{1,0:T(2,128)}, u32[]{:S(2)}) copy-start(s32[2,64]{1,0:T(2,128)} %param.10) | copy-start | bytes 1540
  101.3 96.5 %all-gather.6.cloned.1.call-start = ((), (), s32[]{:S(2)}) async-start(), calls=%async_computation.2 | async-start | bytes 1179648 | tf_op jit(solution)/shard_map/all_gather | solution.py:40
  102.0 162.8 %all-gather.8.cloned.1.call-start = ((), (), s32[]{:S(2)}) async-start(), calls=%async_computation.3 | async-start | bytes 2297856 | tf_op jit(solution)/shard_map/all_gather | solution.py:84
  197.8 4.2 %copy-start.2 = (bf16[64,64,128]{2,1,0:T(8,128)(2,1)S(1)}, bf16[64,64,128]{2,1,0:T(8,128)(2,1)}, u32[]{:S(2)}) copy-start(bf16[64,64,128]{2,1,0:T(8,128)(2,1)} %all-gather.6.cloned.1.call-done) | copy-start | bytes 3145732
  202.1 3.4 %copy-start.1 = (bf16[64,64,256]{2,1,0:T(8,128)(2,1)S(1)}, bf16[64,64,256]{2,1,0:T(8,128)(2,1)}, u32[]{:S(2)}) copy-start(bf16[64,64,256]{2,1,0:T(8,128)(2,1)} %all-gather.4.cloned.1.call-done) | copy-start | bytes 6291460
  216.1 46.9 %copy-start.4 = (bf16[128,50]{0,1:T(8,128)(2,1)S(1)}, bf16[128,50]{0,1:T(8,128)(2,1)}, u32[]{:S(2)}) copy-start(bf16[128,50]{0,1:T(8,128)(2,1)} %param.15) | copy-start | bytes 38404
Sparse Core Ops, SparseCore 0:
  101.4 55.0 all-gather.3
  158.7 39.1 all-gather.5
  203.4 56.2 all-gather.7

commit v2 on v1

--- a/solution.py
+++ b/solution.py
@@ -35,19 +35,29 @@
     slots = group * n_dp
     classes = hyper_out.shape[2]
 
-    ids = lax.all_gather(client_ids, everyone, axis=0, tiled=True)
-    in_group = lax.all_gather(inputs, "hyper", axis=0, tiled=True)
-    in_all = lax.all_gather(in_group, "dp", axis=0, tiled=True)
-    select = (ids[:, None] == jnp.arange(embeddings.shape[0], dtype=jnp.int32)[None, :])
-    picked = jnp.dot(select.astype(bf16), embeddings, preferred_element_type=f32).astype(bf16)
-    hyper_preact = jnp.dot(picked, hyper_in, preferred_element_type=f32) + hyper_bias
-    hidden = jax.nn.silu(hyper_preact).astype(bf16)
+    parts_of_ids = jnp.stack([client_ids // 256, client_ids % 256]).astype(bf16)
+    flat_own = inputs.reshape(own * rows, width_in)
+    packed = jnp.concatenate([flat_own, jnp.pad(parts_of_ids, ((0, 14), (0, width_in - own)))])
+    from_group = lax.all_gather(packed, "hyper", axis=0)
+    from_all = lax.all_gather(from_group, "dp", axis=0)
+    table = jnp.arange(embeddings.shape[0], dtype=jnp.int32)
+
+    def hypernet(gathered):
+        gathered = gathered.reshape(-1, own * rows + 16, width_in)
+        halves = gathered[:, own * rows : own * rows + 2, :own].astype(f32).astype(jnp.int32)
+        ids = (halves[:, 0] * 256 + halves[:, 1]).reshape(-1)
+        select = ids[:, None] == table[None, :]
+        picked = jnp.dot(select.astype(bf16), embeddings, preferred_element_type=f32).astype(bf16)
+        hyper_preact = jnp.dot(picked, hyper_in, preferred_element_type=f32) + hyper_bias
+        hidden = jax.nn.silu(hyper_preact).astype(bf16)
+        return select, picked, hyper_preact, hidden, gathered[:, : own * rows]
+
+    hidden_group, in_group = hypernet(from_group)[3:]
 
     w_wide = lax.dynamic_slice_in_dim(ext_weight, j * wide, wide, 1)
     b_wide = lax.dynamic_slice_in_dim(ext_bias, j * wide, wide, 0).astype(f32)
     preact = jnp.dot(in_group.reshape(group * rows, width_in), w_wide, preferred_element_type=f32)
     features = jax.nn.silu(preact + b_wide).astype(bf16).reshape(group, rows, wide)
-    hidden_group = lax.dynamic_slice_in_dim(hidden, i * group, group, 0)
     heads = jnp.einsum("kh,dhc->kdc", hidden_group, hyper_out, preferred_element_type=f32)
     part = jnp.einsum("krd,kdc->krc", features, heads.astype(bf16), preferred_element_type=f32)
     parts = lax.all_to_all(
@@ -55,12 +65,15 @@
     )
     logits = jnp.sum(parts, axis=0).reshape(own, rows, classes)
     dlogits = class_grads(logits, labels, rows)
+    dlogits, from_all = lax.optimization_barrier((dlogits, from_all))
+    select, picked, hyper_preact, hidden, in_all = hypernet(from_all)
     dl_all = lax.all_gather(dlogits, everyone, axis=0, tiled=True)
 
     start = (j * n_dp + i) * narrow
     w = lax.dynamic_slice_in_dim(ext_weight, start, narrow, 1)
     b = lax.dynamic_slice_in_dim(ext_bias, start, narrow, 0).astype(f32)
     out_rows = lax.dynamic_slice_in_dim(hyper_out, i * narrow, narrow, 0)
+    out_rows = lax.optimization_barrier(out_rows)
     flat = in_all.reshape(slots * rows, width_in)
     preact = jnp.dot(flat, w, preferred_element_type=f32) + b
     features = jax.nn.silu(preact).astype(bf16).reshape(slots, rows, narrow)
@@ -74,15 +87,16 @@
     grad_bias = jnp.sum(dpreact.astype(f32), axis=0)
     grad_out = jnp.einsum("kh,kdc->dhc", hidden, dheads, preferred_element_type=f32)
     dhidden = jnp.einsum("kdc,dhc->kh", dheads, out_rows, preferred_element_type=f32)
-    dhidden = lax.psum(dhidden, everyone)
+    bias_rows = jnp.zeros((n_hyper * n_dp, narrow), f32)
+    bias_rows = lax.dynamic_update_slice_in_dim(bias_rows, grad_bias[None], j * n_dp + i, 0)
+    dhidden, bias_rows = lax.psum((dhidden, bias_rows), everyone)
     hyper_dpre = dhidden * silu_slope(hyper_preact)
     grad_in = jnp.dot(picked.astype(f32).T, hyper_dpre, precision=highest)
     grad_hbias = jnp.sum(hyper_dpre, axis=0)
     back_rows = jnp.dot(hyper_dpre, hyper_in.astype(f32).T, precision=highest)
     grad_table = jnp.dot(select.astype(f32).T, back_rows, precision=highest)
-    both = jnp.concatenate([grad_weight, grad_bias[None]], axis=0)
-    both = lax.all_gather(both, ("hyper", "dp"), axis=1, tiled=True)
-    return (both[:-1], both[-1], grad_table, grad_in, grad_hbias, grad_out)
+    grad_weight = lax.all_gather(grad_weight, ("hyper", "dp"), axis=1, tiled=True)
+    return (grad_weight, bias_rows.reshape(-1), grad_table, grad_in, grad_hbias, grad_out)
 
 
 def solution(mesh):

time: 277 us -> 213 us (0.77)
  blocking collectives: 98.8 us -> 58.7 us
  local copies, waits for them, and re-layouts: 42.4 us -> 27.1 us
  waiting for transfers between devices: 55.1 us -> 44.1 us
    unnamed x1 -> x0, blocking collectives: 42 us -> none
    all_gather x2, waiting for transfers between devices: 33.7 us -> 0.01 us  [the longest x1 0.01 us: local(): from_all = lax.all_gather(from_group, 'dp', axis=0)]
    unnamed x16 -> x24, local copies, waits for them, and re-layouts: 33.5 us -> 9.45 us
    all_gather x1, waiting for transfers between devices: 20.6 us -> 44.1 us  [local(): dl_all = lax.all_gather(dlogits, everyone, axis=0, tiled=True)]
    optimization_barrier x0 -> x1, local copies, waits for them, and re-layouts: none -> 6.44 us  [local(): out_rows = lax.optimization_barrier(out_rows)]
    slice x2, local copies, waits for them, and re-layouts: 4.63 us -> 0.12 us  [hypernet(): return (select, picked, hyper_preact, hidden, gathered[:, :own * rows])]
    dynamic_slice x0 -> x1, local copies, waits for them, and re-layouts: none -> 4.12 us  [local(): out_rows = lax.dynamic_slice_in_dim(hyper_out, i * narrow, narrow, 0)]
    convert_element_type x2 -> x1, local copies, waits for them, and re-layouts: 4.08 us -> 6.61 us  [local(): jnp.einsum('krd,krc->kdc', features, dl_all, preferred_element_type=f32)]
  transfers between devices with their start and end apart: 3 -> 3, of which waited for: 2 -> 1; matrix products, arithmetic and copies ran while one was open for 23% -> 38% of each run, Pallas kernels for 0% -> 0%
where the time goes in v2:
time: 213 us
  matrix products  63.2 us (30%)
  blocking collectives  58.7 us (28%)
  waiting for transfers between devices  44.1 us (21%)
  local copies, waits for them, and re-layouts  27.1 us (13%)
  between operations  13.9 us (7%)
  other arithmetic  5.5 us (3%)
    all_gather x1, waiting for transfers between devices, local(): dl_all = lax.all_gather(dlogits, everyone, axis=0, tiled=True)  44.1 us
    psum x1, blocking collectives, local(): dhidden, bias_rows = lax.psum((dhidden, bias_rows), everyone)  39.9 us
    dot_general x1, matrix products, local(): jnp.einsum('kh,dhc->kdc', hidden_group, hyper_out, preferred_element_type...  29.1 us
    all_to_all x1, blocking collectives, local(): lax.all_to_all(part.reshape(n_hyper, own * rows, classes), 'hyper', split...  11.7 us
    unnamed x24, local copies, waits for them, and re-layouts  9.45 us
    all_gather x1, blocking collectives, local(): from_group = lax.all_gather(packed, 'hyper', axis=0)  7.06 us
    dot_general x1, matrix products, local(): jnp.einsum('kh,dhc->kdc', hidden, out_rows, preferred_element_type=f32)  7.02 us
    convert_element_type x1, local copies, waits for them, and re-layouts, local(): jnp.einsum('krd,krc->kdc', features, dl_all, preferred_element_type=f32)  6.61 us
  transfers between devices with their start and end apart: 3, of which 1 were waited for; matrix products, arithmetic and copies ran while one was open for 38% of the time, Pallas kernels for 0%

profile of v2, /device:TPU:0, one launch (start us, length us, event | category | flops | bytes accessed | tf_op | source)
XLA Modules:
  0.0 212.7 jit_solution(18060032566630711155)
XLA Ops:
  7.2 0.0 copy-start
  7.2 0.0 all-gather.10.cloned.1.call-start
  7.2 0.7 convert_bitcast_fusion
  8.0 0.8 pad_maximum_fusion
  8.8 7.1 %all-gather = bf16[576,128]{1,0:T(8,128)(2,1)} all-gather(bf16[144,128]{1,0:T(8,128)(2,1)S(1)} %pad_maximum_fusion), channel_id=2, replica_groups=mesh['dp'=8,'hyper'=4] {'hyper'}, dimensions={0}, use_global_device_ids=true | all-gather | bytes 184320 | tf_op jit(solution)/shard_map/all_gather | solution.py:41
  15.8 0.0 all-gather.10.cloned.1.call-update
  15.8 0.0 all-gather.6.cloned.1.call-start
  15.9 0.7 convert_convert_fusion.1
  16.6 0.1 add.113
  16.7 1.0 fusion.37
  17.7 29.1 %fusion.16 = bf16[8,1024,256]{2,0,1:T(8,128)(2,1)} fusion(bf16[8,50,1]{1,0,2:T(8,128)(2,1)S(1)} %fusion.37, bf16[1024,50,256]{2,0,1:T(8,128)(2,1)} %param.17), kind=kOutput, calls=%fused_computation.13 | convolution fusion | flops 211812352 | bytes 30409504 | tf_op jit(solution)/shard_map/kh,dhc->kdc/dot_general | solution.py:61
  46.8 0.7 dynamic-slice_convert_fusion
  47.5 0.7 multiply_convert_fusion.1
  48.3 1.5 copy-done.3
  49.7 0.9 fusion.6
  50.6 11.7 %all_to_all.5 = f32[4,128,256]{2,1,0:T(8,128)S(1)} all-to-all(f32[4,128,256]{2,1,0:T(8,128)S(1)} %bitcast.59), channel_id=1, replica_groups=mesh['dp'=8,'hyper'=4] {'hyper'}, dimensions={0} | all-to-all | bytes 1048576 | tf_op jit(solution)/shard_map/all_to_all | solution.py:63
  62.4 0.1 reduce_max.9
  62.5 0.1 sub.29
  62.5 0.2 exponential_reduce_fusion
  62.7 0.1 div.52
  62.8 0.8 multiply_convert_fusion.2
  63.6 0.0 all-gather.6.cloned.1.call-update
  63.6 0.0 all-gather.8.cloned.1.call-start
  63.7 4.1 %constant_dynamic-slice_fusion = bf16[128,50,256]{2,0,1:T(8,128)(2,1)} fusion(bf16[1024,50,256]{2,0,1:T(8,128)(2,1)} %param.17, s32[]{:T(128)S(6)} %select_n.29), kind=kLoop, calls=%fused_computation.69 | loop fusion | bytes 6553604 | tf_op jit(solution)/shard_map/dynamic_slice | solution.py:75
  67.8 0.8 dynamic-slice_convert_fusion.1
  68.6 0.1 slice.36
  68.7 0.1 fusion.26
  68.8 0.1 add.118
  68.9 0.2 convolution_convert_fusion.1
  69.1 0.1 convolution_add_fusion.1
  69.2 7.0 %fusion.13 = bf16[64,128,256]{2,0,1:T(8,128)(2,1)} fusion(bf16[128,50,256]{2,0,1:T(8,128)(2,1)} %constant_dynamic-slice_fusion, f32[64,50]{0,1:T(8,128)S(1)} %convolution_add_fusion.1), kind=kOutput, calls=%fused_computation.12 | convolution fusion | flops 211828352 | bytes 7483904 | tf_op jit(solution)/shard_map/kh,dhc->kdc/dot_general | solution.py:80
  76.2 44.1 %all-gather.6.cloned.1.call-done = bf16[64,64,256]{2,1,0:T(8,128)(2,1)} async-done(((bf16[2,64,256]{2,1,0:T(8,128)(2,1)}), bf16[64,64,256]{2,1,0:T(8,128)(2,1)}) %all-gather.6.cloned.1.call-update) | async-done | bytes 2097168 | tf_op jit(solution)/shard_map/all_gather | solution.py:70
  120.3 5.5 %fusion.20 = bf16[64,64,128]{2,1,0:T(8,128)(2,1)S(1)} fusion(bf16[64,64,256]{2,1,0:T(8,128)(2,1)} %all-gather.6.cloned.1.call-done, bf16[64,128,256]{2,0,1:T(8,128)(2,1)} %fusion.13), kind=kOutput, calls=%fused_computation.21 | convolution fusion | flops 268959744 | bytes 7340032 | tf_op jit(solution)/shard_map/krc,kdc->krd/dot_general | solution.py:82
  125.8 2.3 %convert_reduce_fusion = (f32[128]{0:T(128)S(1)}, bf16[4096,128]{1,0:T(8,128)(2,1)S(1)}, bf16[4096,128]{1,0:T(8,128)(2,1)}) fusion(bf16[64,64,128]{2,1,0:T(8,128)(2,1)S(1)} %fusion.20, f32[128]{0:T(128)S(1)} %dynamic-slice_convert_fusion.1, bf16[4096,128]{1,0:T(8,128)(2,1)S(1)} %bitcast.52, bf16[128,4096]{1,0:T(8,128)(2,1)S(1)} %copy-done, s32[]{:T(128)S(6)} %select_n.30), kind=kOutput, calls=%fused_computation.18 | convolution fusion | flops 142081920 | bytes 4228100 | tf_op jit(solution)/shard_map/dot_general | solution.py:78
  128.1 1.1 fusion.47
  129.3 0.0 all-gather.8.cloned.1.call-update
  129.3 6.4 %copy.28 = bf16[128,50,256]{0,1,2:T(8,128)(2,1)} copy(bf16[128,50,256]{2,0,1:T(8,128)(2,1)} %constant_dynamic-slice_fusion) | data formatting | bytes 6553600 | tf_op jit(solution)/shard_map/optimization_barrier | solution.py:76
  135.8 3.3 %convolution_convert_fusion = bf16[64,128,256]{2,1,0:T(8,128)(2,1)} fusion(bf16[64,64,128]{2,1,0:T(8,128)(2,1)S(1)} %bitcast.58, bf16[64,64,256]{2,1,0:T(8,128)(2,1)S(1)} %copy-done.2), kind=kOutput, calls=%fused_computation.14 | convolution fusion | flops 270532608 | bytes 7340032 | tf_op jit(solution)/shard_map/krd,krc->kdc/dot_general | solution.py:81
  139.1 6.6 %copy.27 = bf16[64,128,256]{1,0,2:T(8,128)(2,1)} copy(bf16[64,128,256]{2,1,0:T(8,128)(2,1)} %convolution_convert_fusion) | data formatting | bytes 8388608 | tf_op jit(solution)/shard_map/convert_element_type | solution.py:81
  145.7 5.4 %fusion.10 = f32[128,50,256]{2,1,0:T(8,128)S(1)} fusion(bf16[64,128,256]{2,1,0:T(8,128)(2,1)} %convolution_convert_fusion, f32[64,50]{0,1:T(8,128)S(1)} %convolution_add_fusion.1), kind=kOutput, calls=%fused_computation.11 | convolution fusion | flops 209731200 | bytes 10760704 | tf_op jit(solution)/shard_map/kh,kdc->dhc/dot_general | solution.py:88
  151.1 4.8 %copy.30 = f32[128,50,256]{2,0,1:T(8,128)} copy(f32[128,50,256]{2,1,0:T(8,128)S(1)} %fusion.10) | data formatting | bytes 13107200
  155.9 4.6 %convolution_bitcast_fusion = f32[64,50]{0,1:T(8,128)S(1)} fusion(bf16[64,128,256]{1,0,2:T(8,128)(2,1)} %copy.27, bf16[128,50,256]{0,1,2:T(8,128)(2,1)} %copy.28), kind=kOutput, calls=%fused_computation.22 | convolution fusion | flops 209715200 | bytes 7483904 | tf_op jit(solution)/shard_map/kdc,dhc->kh/dot_general | solution.py:89
  160.6 39.9 %all-reduce.1 = (f32[4096]{0:T(1024)}, f32[64,50]{0,1:T(8,128)S(1)}) all-reduce(f32[4096]{0:T(1024)S(1)} %bitcast.61, f32[64,50]{0,1:T(8,128)S(1)} %convolution_bitcast_fusion), channel_id=1, replica_groups=mesh['dp'=8,'hyper'=4] {'dp','hyper'}, use_global_device_ids=true, to_apply=%region_4.5 | all-reduce | flops 7296 | bytes 58368 | tf_op jit(solution)/shard_map/psum | solution.py:92
  200.5 0.6 fusion.45
  201.1 0.2 fusion.48
  201.4 0.9 fusion.25
  202.3 0.8 fusion.49
  203.0 3.1 %copy.51 = f32[128,4096]{1,0:T(8,128)} copy(f32[128,4096]{1,0:T(8,128)} %all-gather.8.cloned.1.call-done) | data formatting | bytes 4194304
  (29 shorter events, 0.2 us)
Async XLA Ops:
  7.2 40.4 %copy-start = (bf16[128,4096]{1,0:T(8,128)(2,1)S(1)}, bf16[128,4096]{1,0:T(8,128)(2,1)}, u32[]{:S(2)}) copy-start(bf16[128,4096]{1,0:T(8,128)(2,1)} %param.12) | copy-start | bytes 3145732
  7.2 56.4 %all-gather.10.cloned.1.call-start = ((), (), s32[]{:S(2)}) async-start(), calls=%async_computation.3 | async-start | bytes 1327104 | tf_op jit(solution)/shard_map/all_gather | solution.py:42
  15.8 104.5 %all-gather.6.cloned.1.call-start = ((), (), s32[]{:S(2)}) async-start(), calls=%async_computation.1 | async-start | bytes 2162688 | tf_op jit(solution)/shard_map/all_gather | solution.py:70
  17.7 29.1 %copy-start.4 = (bf16[576,128]{1,0:T(8,128)(2,1)S(1)}, bf16[576,128]{1,0:T(8,128)(2,1)}, u32[]{:S(2)}) copy-start(bf16[576,128]{1,0:T(8,128)(2,1)} %all-gather) | copy-start | bytes 442372
  47.5 2.2 %copy-start.3 = (bf16[8,1024,256]{2,0,1:T(8,128)(2,1)S(1)}, bf16[8,1024,256]{2,0,1:T(8,128)(2,1)}, u32[]{:S(2)}) copy-start(bf16[8,1024,256]{2,0,1:T(8,128)(2,1)} %fusion.16) | copy-start | bytes 12582916
  49.7 13.1 %copy-start.8 = (s32[2,64]{1,0:T(2,128)S(1)}, s32[2,64]{1,0:T(2,128)}, u32[]{:S(2)}) copy-start(s32[2,64]{1,0:T(2,128)} %param.10) | copy-start | bytes 1540
  63.6 139.4 %all-gather.8.cloned.1.call-start = ((), (), s32[]{:S(2)}) async-start(), calls=%async_computation.2 | async-start | bytes 2162688 | tf_op jit(solution)/shard_map/all_gather | solution.py:98
  63.7 4.9 %copy-start.6 = (bf16[32,144,128]{2,1,0:T(8,128)(2,1)S(1)}, bf16[32,144,128]{2,1,0:T(8,128)(2,1)}, u32[]{:S(2)}) copy-start(bf16[32,144,128]{2,1,0:T(8,128)(2,1)} %all-gather.10.cloned.1.call-done) | copy-start | bytes 3538948
  63.7 5.2 %copy-start.9 = (bf16[64,128]{1,0:T(8,128)(2,1)S(1)}, bf16[64,128]{1,0:T(8,128)(2,1)}, u32[]{:S(2)}) copy-start(bf16[64,128]{1,0:T(8,128)(2,1)} %param.14) | copy-start | bytes 49156
  63.7 5.4 %copy-start.7 = (bf16[128,50]{0,1:T(8,128)(2,1)S(1)}, bf16[128,50]{0,1:T(8,128)(2,1)}, u32[]{:S(2)}) copy-start(bf16[128,50]{0,1:T(8,128)(2,1)} %param.15) | copy-start | bytes 38404
  63.7 5.4 %copy-start.10 = (f32[50]{0:T(128)S(1)}, f32[50]{0:T(128)}, u32[]{:S(2)}) copy-start(f32[50]{0:T(128)} %param.16) | copy-start | bytes 604
  129.3 6.5 %copy-start.2 = (bf16[64,64,256]{2,1,0:T(8,128)(2,1)S(1)}, bf16[64,64,256]{2,1,0:T(8,128)(2,1)}, u32[]{:S(2)}) copy-start(bf16[64,64,256]{2,1,0:T(8,128)(2,1)} %all-gather.6.cloned.1.call-done) | copy-start | bytes 6291460
  129.3 6.5 %copy-start.5 = (bf16[4096,128]{1,0:T(8,128)(2,1)S(1)}, bf16[4096,128]{1,0:T(8,128)(2,1)}, u32[]{:S(2)}) copy-start(bf16[4096,128]{1,0:T(8,128)(2,1)} %get-tuple-element.34) | copy-start | bytes 3145732
  155.9 50.2 %copy-start.1 = (bf16[128,4096]{1,0:T(8,128)(2,1)S(1)}, bf16[128,4096]{1,0:T(8,128)(2,1)}, u32[]{:S(2)}) copy-start(bf16[128,4096]{1,0:T(8,128)(2,1)} %param.12) | copy-start | bytes 3145732
Sparse Core Ops, SparseCore 0:
  16.0 42.6 all-gather.9
  63.7 56.5 all-gather.5
  129.4 55.5 all-gather.7
